TPU v7x, 32 devices: a whole 2x2x4 slice. The times are simulated.
32 devices in a mesh: rep: 4 (over z), row: 2 (over x), col: 4 (over y, core).
Axes of the slice: x: 2, y: 2, z: 4, core: 2. Of those that a mesh axis runs over, the one named last changes fastest.
Arguments:
- grad_parts: bfloat16 [4, 8192, 8192], P('rep', 'row', 'col'), may hold values from -6 to 6
- momentum: float32 [8192, 8192], P(('row', 'rep'), 'col'), may hold values from -24 to 24
- basis: float32 [8192, 384], P('col'), may hold values from -0.0625 to 0.0625
Outputs:
- update: bfloat16 [8192, 8192], P('row', 'col')
- new_momentum: float32 [8192, 8192], P(('row', 'rep'), 'col')
- new_basis: float32 [8192, 384], P('col')
- power_norms: float32 [384], replicated
All inputs are finite; a program needn't handle non-finite values.
Results may differ from a plain program's by a relative error of at most 0.0085.
Values may be sent and summed in bfloat16 or wider, within the bound.
No kernel may reach another device: no remote copies, remote signals or barrier semaphores. Data moves between devices by JAX's collectives and lax.ppermute only.
A program may use at most 128 MiB of HBM per device.

v0:
```python
import jax
import jax.numpy as jnp
from jax import lax
from jax.sharding import PartitionSpec as P

D = 8192
RANK = 384
EPS = 1e-06
FEEDBACK = 0.05
HIGH = lax.Precision.HIGHEST


def local(grad_parts, momentum, basis):
    replicas = lax.axis_size("rep")
    local_grad = grad_parts[0].astype(jnp.float32)
    summed = lax.psum_scatter(
        local_grad.astype(jnp.bfloat16), "rep", scatter_dimension=0, tiled=True
    ).astype(jnp.float32)
    blended = momentum + summed / replicas
    power = jnp.dot(blended, basis, precision=HIGH)
    power = lax.psum(power, "col")
    squares = lax.psum(jnp.sum(power * power, axis=0), ("rep", "row"))
    power_norms = jnp.sqrt(squares / D)
    scaled = power / (jnp.sqrt(squares) + EPS)
    gram = lax.psum(jnp.dot(scaled.T, scaled, precision=HIGH), ("rep", "row"))
    factor = jnp.linalg.cholesky(gram)
    orth = jax.scipy.linalg.solve_triangular(factor, scaled.T, lower=True).T
    tile_orth = lax.all_gather(orth, "rep", axis=0, tiled=True)
    back = jnp.dot(blended.T, orth, precision=HIGH)
    back = lax.psum(back, ("rep", "row"))
    back_squares = lax.psum(jnp.sum(back * back, axis=0), "col")
    new_basis = back / (jnp.sqrt(back_squares) + EPS)
    new_momentum = blended - FEEDBACK * jnp.dot(orth, back.T, precision=HIGH)
    scale = D / RANK**0.5
    update = (scale * jnp.dot(tile_orth, new_basis.T, precision=HIGH)).astype(jnp.bfloat16)
    return (update, new_momentum, new_basis, power_norms)


def solution(mesh):
    placed = (P("rep", "row", "col"), P(("row", "rep"), "col"), P("col", None))
    return jax.shard_map(
        local,
        mesh=mesh,
        in_specs=placed,
        out_specs=(P("row", "col"), P(("row", "rep"), "col"), P("col", None), P()),
        check_vma=False,
    )
```

profile of v0, /device:TPU:0, one launch (start us, length us, event | category | flops | bytes accessed | tf_op | source)
XLA Modules:
  0.0 922.6 jit_solution(1023822813130225376)
XLA Ops:
  7.2 0.0 copy-start
  7.2 0.0 reduce-scatter.2.cloned.1.call-start
  7.2 0.7 reduce-scatter.2.cloned.1.call-update
  7.9 0.0 all-reduce.5.cloned.1.call-start
  8.0 285.6 %reduce-scatter.2.cloned.1.call-done = bf16[1024,2048]{1,0:T(8,128)(2,1)} async-done(((bf16[4096,2048]{1,0:T(8,128)(2,1)}), bf16[1024,2048]{1,0:T(8,128)(2,1)}) %reduce-scatter.2.cloned.1.call-update) | async-done | bytes 4194320 | tf_op jit(solution)/shard_map/reduce_scatter | solution.py:16
  293.5 17.7 %fusion.1 = f32[1024,384]{1,0:T(8,128)} fusion(f32[2048,384]{1,0:T(8,128)S(1)} %copy-done, f32[1024,2048]{1,0:T(8,128)} %param.4, bf16[1024,2048]{1,0:T(8,128)(2,1)} %reduce-scatter.2.cloned.1.call-done), kind=kOutput, calls=%fused_computation.7 | convolution fusion | flops 9669967872 | bytes 17301504 | tf_op jit(solution)/shard_map/dot_general | solution.py:20
  311.3 0.0 all-reduce.5.cloned.1.call-update
  311.3 0.0 all-reduce.7.cloned.1.call-start
  311.3 43.6 %all-reduce.5.cloned.1.call-done = f32[1024,384]{1,0:T(8,128)} async-done(((f32[1024,384]{1,0:T(8,128)}), f32[1024,384]{1,0:T(8,128)}) %all-reduce.5.cloned.1.call-update) | async-done | bytes 1572880 | tf_op jit(solution)/shard_map/psum | solution.py:21
  354.9 1.6 multiply_reduce_fusion.1
  356.5 21.4 %psum.36 = f32[384]{0:T(512)S(1)} all-reduce(f32[384]{0:T(512)S(1)} %multiply_reduce_fusion.1), channel_id=1, replica_groups=mesh['rep'=4,'row'=2,'col'=4] {'rep','row'}, use_global_device_ids=true, to_apply=%region_3.0 | all-reduce | flops 384 | bytes 3072 | tf_op jit(solution)/shard_map/psum | solution.py:22
  377.9 0.6 multiply_sqrt_fusion
  378.5 5.6 fusion.7
  384.0 0.0 all-reduce.7.cloned.1.call-update
  384.0 0.2 all-reduce.9.cloned.1.call-start
  384.3 0.1 fusion.6
  384.4 69.4 %all-reduce.7.cloned.1.call-done = f32[384,384]{0,1:T(8,128)} async-done(((f32[384,384]{0,1:T(8,128)}), f32[384,384]{0,1:T(8,128)}) %all-reduce.7.cloned.1.call-update) | async-done | bytes 589840 | tf_op jit(solution)/shard_map/psum | solution.py:25
  453.9 1.3 copy.8
  455.1 1.1 fusion.8
  456.3 11.7 %cholesky.77 = f32[128,128]{1,0:T(8,128)S(1)} custom-call(f32[128,128]{1,0:T(8,128)S(1)} %cholesky.192), custom_call_target="Cholesky" | custom-call | tf_op jit(solution)/shard_map/jit(cholesky)/cholesky | solution.py:26
  468.0 9.8 %custom-call.23 = f32[1,128,128]{1,2,0:T(8,128)S(1)} custom-call(f32[1,128,128]{2,1,0:T(8,128)S(1)} %get-tuple-element.28), custom_call_target="InvertDiagBlocksLowerTriangular" | custom-call | tf_op jit(solution)/shard_map/jit(cholesky)/cholesky | solution.py:26
  477.9 0.3 constant_dynamic-update-slice_fusion.2
  478.2 0.3 convolution_subtract_fusion.2
  478.5 11.7 %cholesky.162 = f32[128,128]{1,0:T(8,128)S(1)} custom-call(f32[128,128]{1,0:T(8,128)S(1)} %cholesky.196), custom_call_target="Cholesky" | custom-call | tf_op jit(solution)/shard_map/jit(cholesky)/cholesky | solution.py:26
  490.2 10.2 %custom-call.24 = f32[1,128,128]{1,2,0:T(8,128)S(1)} custom-call(f32[1,128,128]{2,1,0:T(8,128)S(1)} %get-tuple-element.25), custom_call_target="InvertDiagBlocksLowerTriangular" | custom-call | tf_op jit(solution)/shard_map/jit(cholesky)/cholesky | solution.py:26
  500.4 0.2 convolution_dynamic-update-slice_fusion
  500.6 0.3 convolution_subtract_fusion.3
  500.9 11.7 %cholesky.181 = f32[128,128]{1,0:T(8,128)S(1)} custom-call(f32[128,128]{1,0:T(8,128)S(1)} %convolution_subtract_fusion.3), custom_call_target="Cholesky" | custom-call | tf_op jit(solution)/shard_map/jit(cholesky)/cholesky | solution.py:26
  512.7 0.7 compare_reduce_fusion
  513.4 0.6 compare_reduce_fusion.1
  516.1 6.0 while.1
  516.1 0.1 constant_dynamic-slice_fusion.2
  516.2 0.5 fusion.37
  516.7 1.4 bitcast_dynamic-update-slice_fusion.2
  518.1 0.1 constant_dynamic-slice_fusion.2
  518.2 0.5 fusion.37
  518.7 1.4 bitcast_dynamic-update-slice_fusion.2
  520.1 0.1 constant_dynamic-slice_fusion.2
  520.2 0.5 fusion.37
  520.7 1.4 bitcast_dynamic-update-slice_fusion.2
  522.1 0.0 copy-start.12
  522.1 29.5 %custom-call.25 = f32[3,128,128]{1,2,0:T(8,128)S(1)} custom-call(f32[3,128,128]{2,1,0:T(8,128)S(1)} %get-tuple-element.11), custom_call_target="InvertDiagBlocksLowerTriangular" | custom-call | tf_op jit(solution)/shard_map/jit(_solve_triangular)/triangular_solve | solution.py:27
  551.6 0.6 fusion.9
  552.3 1.0 convolution_subtract_fusion.1
  553.3 0.6 fusion.17
  553.9 2.9 convolution_subtract_fusion
  556.8 0.6 fusion.15
  557.5 30.4 %fusion = f32[2048,384]{1,0:T(8,128)} fusion(f32[1024,2048]{1,0:T(8,128)} %param.4, bf16[1024,2048]{1,0:T(8,128)(2,1)S(1)} %copy-done.2, f32[128,1024]{1,0:T(8,128)S(1)} %fusion.15, f32[128,1024]{1,0:T(8,128)S(1)} %fusion.17, f32[128,1024]{1,0:T(8,128)S(1)} %fusion.9), kind=kOutput, calls=%fused_computation.6 | convolution fusion | flops 9670754304 | bytes 17301504 | tf_op jit(solution)/shard_map/dot_general | solution.py:29
  587.8 0.0 all-reduce.9.cloned.1.call-update
  587.9 0.0 all-gather.2.cloned.1.call-start
  588.0 1.3 fusion.5
  589.3 0.0 all-gather.2.cloned.1.call-update
  589.3 126.5 %all-reduce.9.cloned.1.call-done = f32[2048,384]{1,0:T(8,128)} async-done(((f32[2048,384]{1,0:T(8,128)}), f32[2048,384]{1,0:T(8,128)}) %all-reduce.9.cloned.1.call-update) | async-done | bytes 3145744 | tf_op jit(solution)/shard_map/psum | solution.py:30
  715.8 2.3 multiply_reduce_fusion
  718.1 6.2 psum.39
  724.4 0.0 copy-start.10
  724.4 1.9 broadcast_divide_fusion
  726.3 1.7 copy-done.3
  728.0 0.2 copy-done.6
  728.1 0.2 copy-done.8
  728.4 0.2 copy-done.10
  728.6 23.8 %multiply_subtract_fusion = f32[1024,2048]{1,0:T(8,128)} fusion(f32[2048,384]{1,0:T(8,128)S(1)} %copy-done.4, f32[1024,2048]{1,0:T(8,128)} %param.4, bf16[1024,2048]{1,0:T(8,128)(2,1)S(1)} %copy-done.3, f32[128,1024]{1,0:T(8,128)S(1)} %copy-done.10, f32[128,1024]{1,0:T(8,128)S(1)} %copy-done.8, f32[128,1024]{1,0:T(8,128)S(1)} %copy-done.6), kind=kOutput, calls=%fused_computation.3 | convolution fusion | flops 9674948608 | bytes 25690112 | tf_op jit(solution)/shard_map/dot_general | solution.py:33
  752.3 79.8 %all-gather.2.cloned.1.call-done = f32[4096,384]{0,1:T(8,128)} async-done(((f32[1024,384]{0,1:T(8,128)}), f32[4096,384]{0,1:T(8,128)}) %all-gather.2.cloned.1.call-update) | async-done | bytes 6291472 | tf_op jit(solution)/shard_map/all_gather | solution.py:28
  832.2 83.8 %multiply_convert_fusion = bf16[4096,2048]{1,0:T(8,128)(2,1)} fusion(f32[4096,384]{0,1:T(8,128)} %all-gather.2.cloned.1.call-done, f32[2048,384]{1,0:T(8,128)} %broadcast_divide_fusion), kind=kOutput, calls=%fused_computation.2 | convolution fusion | flops 38671482880 | bytes 26214400 | tf_op jit(solution)/shard_map/dot_general | solution.py:35
  (30 shorter events, 0.3 us)
Async XLA Ops:
  7.2 286.4 %copy-start = (f32[2048,384]{1,0:T(8,128)S(1)}, f32[2048,384]{1,0:T(8,128)}, u32[]{:S(2)}) copy-start(f32[2048,384]{1,0:T(8,128)} %param.5) | copy-start | bytes 9437188
  7.2 286.4 %reduce-scatter.2.cloned.1.call-start = ((), (), s32[]{:S(2)}) async-start(), calls=%async_computation.1 | async-start | bytes 20971520 | tf_op jit(solution)/shard_map/reduce_scatter | solution.py:16
  7.9 347.0 %all-reduce.5.cloned.1.call-start = ((), (), s32[]{:S(2)}) async-start(), calls=%async_computation.2 | async-start | bytes 3145728 | tf_op jit(solution)/shard_map/psum | solution.py:21
  311.3 142.6 %all-reduce.7.cloned.1.call-start = ((), (), s32[]{:S(2)}) async-start(), calls=%async_computation.3 | async-start | bytes 1179648 | tf_op jit(solution)/shard_map/psum | solution.py:25
  378.5 5.8 copy-start.11
  384.0 331.7 %all-reduce.9.cloned.1.call-start = ((), (), s32[]{:S(2)}) async-start(), calls=%async_computation.5 | async-start | bytes 6291456 | tf_op jit(solution)/shard_map/psum | solution.py:30
  522.1 30.2 %copy-start.12 = (f32[384,384]{1,0:T(8,128)}, f32[384,384]{1,0:T(8,128)S(1)}, u32[]{:S(2)}) copy-start(f32[384,384]{1,0:T(8,128)S(1)} %get-tuple-element.96) | copy-start | bytes 1769476
  552.3 35.7 %copy-start.5 = (f32[128,1024]{1,0:T(8,128)}, f32[128,1024]{1,0:T(8,128)S(1)}, u32[]{:S(2)}) copy-start(f32[128,1024]{1,0:T(8,128)S(1)} %fusion.9) | copy-start | bytes 1572868
  552.3 5.2 copy-start.2
  553.9 34.0 %copy-start.7 = (f32[128,1024]{1,0:T(8,128)}, f32[128,1024]{1,0:T(8,128)S(1)}, u32[]{:S(2)}) copy-start(f32[128,1024]{1,0:T(8,128)S(1)} %fusion.17) | copy-start | bytes 1572868
  557.5 30.5 %copy-start.9 = (f32[128,1024]{1,0:T(8,128)}, f32[128,1024]{1,0:T(8,128)S(1)}, u32[]{:S(2)}) copy-start(f32[128,1024]{1,0:T(8,128)S(1)} %fusion.15) | copy-start | bytes 1572868
  587.9 244.3 %all-gather.2.cloned.1.call-start = ((), (), s32[]{:S(2)}) async-start(), calls=%async_computation.4 | async-start | bytes 7864320 | tf_op jit(solution)/shard_map/all_gather | solution.py:28
  715.8 8.6 copy-start.4
  724.3 3.6 copy-start.3
  724.4 3.8 copy-start.6
  724.4 4.0 copy-start.8
  724.4 4.2 copy-start.10
  832.2 83.8 %copy-start.1 = (f32[2048,384]{1,0:T(8,128)S(1)}, f32[2048,384]{1,0:T(8,128)}, u32[]{:S(2)}) copy-start(f32[2048,384]{1,0:T(8,128)} %param.5) | copy-start | bytes 9437188
Sparse Core Ops, SparseCore 0:
  10.3 283.1 reduce-scatter.1
  311.4 43.4 all-reduce.4
  384.2 69.6 all-reduce.6
  588.0 127.7 all-reduce.8
  717.8 114.3 all-gather.1
where the time goes:
time: 930 us; the launch traced here: 923 us
  waiting for transfers between devices  606 us (65%)
  matrix products  168 us (18%)
  other arithmetic  95.1 us (10%)
  blocking collectives  27.6 us (3%)
  between operations  16.3 us (2%)
  local copies, waits for them, and re-layouts  9.64 us (1%)
    reduce_scatter x1, waiting for transfers between devices, local(): lax.psum_scatter(local_grad.astype(jnp.bfloat16), 'rep', scatter_dimensio...  286 us
    psum x1, waiting for transfers between devices, local(): back = lax.psum(back, ('rep', 'row'))  126 us
    dot_general x1, matrix products, local(): jnp.dot(tile_orth, new_basis.T, precision=HIGH)  83.8 us
    all_gather x1, waiting for transfers between devices, local(): tile_orth = lax.all_gather(orth, 'rep', axis=0, tiled=True)  79.8 us
    psum x1, waiting for transfers between devices, local(): gram = lax.psum(jnp.dot(scaled.T, scaled, precision=HIGH), ('rep', 'row'))  69.4 us
    another operation x10, other arithmetic, local(): factor = jnp.linalg.cholesky(gram)  56.6 us
    psum x1, waiting for transfers between devices, local(): power = lax.psum(power, 'col')  43.6 us
    dot_general x1, matrix products, local(): back = jnp.dot(blended.T, orth, precision=HIGH)  30.4 us
  transfers between devices with their start and end apart: 5, of which 5 were waited for; matrix products, arithmetic and copies ran while one was open for 3% of the time, Pallas kernels for 0%

commit v1 on v0

--- a/solution.py
+++ b/solution.py
@@ -25,7 +25,12 @@
     gram = lax.psum(jnp.dot(scaled.T, scaled, precision=HIGH), ("rep", "row"))
     factor = jnp.linalg.cholesky(gram)
     orth = jax.scipy.linalg.solve_triangular(factor, scaled.T, lower=True).T
-    tile_orth = lax.all_gather(orth, "rep", axis=0, tiled=True)
+    ring = [orth]
+    for hop in range(3):
+        ring.append(lax.ppermute(ring[-1], "rep", [(dev, (dev + 1) % 4) for dev in range(4)]))
+    tile_orth = jnp.roll(
+        jnp.concatenate(ring[::-1], axis=0), (lax.axis_index("rep") + 1) * ring[0].shape[0], axis=0
+    )
     back = jnp.dot(blended.T, orth, precision=HIGH)
     back = lax.psum(back, ("rep", "row"))
     back_squares = lax.psum(jnp.sum(back * back, axis=0), "col")

time: 930 us -> 909 us (0.977)
  waiting for transfers between devices: 606 us -> 584 us
    all_gather x1 -> x0, waiting for transfers between devices: 79.8 us -> none  [local(): tile_orth = lax.all_gather(orth, 'rep', axis=0, tiled=True)]
    ppermute x0 -> x3, waiting for transfers between devices: none -> 75.9 us  [local(): lax.ppermute(ring[-1], 'rep', [(dev, (dev + 1) % 4) for dev in range(4)])]
    psum x1, waiting for transfers between devices: 126 us -> 108 us  [local(): back = lax.psum(back, ('rep', 'row'))]
  transfers between devices with their start and end apart: 5 -> 7, of which waited for: 5 -> 6; matrix products, arithmetic and copies ran while one was open for 3% -> 3% of each run, Pallas kernels for 0% -> 0%
where the time goes in v1:
time: 909 us; the launch traced here: 902 us
  waiting for transfers between devices  584 us (64%)
  matrix products  167 us (18%)
  other arithmetic  94.3 us (10%)
  blocking collectives  27.6 us (3%)
  between operations  16.2 us (2%)
  local copies, waits for them, and re-layouts  11.8 us (1%)
    reduce_scatter x1, waiting for transfers between devices, local(): lax.psum_scatter(local_grad.astype(jnp.bfloat16), 'rep', scatter_dimensio...  286 us
    psum x1, waiting for transfers between devices, local(): back = lax.psum(back, ('rep', 'row'))  108 us
    dot_general x1, matrix products, local(): jnp.dot(tile_orth, new_basis.T, precision=HIGH)  81.5 us
    ppermute x3, waiting for transfers between devices, local(): lax.ppermute(ring[-1], 'rep', [(dev, (dev + 1) % 4) for dev in range(4)])  75.9 us
    psum x1, waiting for transfers between devices, local(): gram = lax.psum(jnp.dot(scaled.T, scaled, precision=HIGH), ('rep', 'row'))  69.4 us
    another operation x10, other arithmetic, local(): factor = jnp.linalg.cholesky(gram)  56.5 us
    psum x1, waiting for transfers between devices, local(): power = lax.psum(power, 'col')  43.6 us
    dot_general x1, matrix products, local(): back = jnp.dot(blended.T, orth, precision=HIGH)  30.4 us
  transfers between devices with their start and end apart: 7, of which 6 were waited for; matrix products, arithmetic and copies ran while one was open for 3% of the time, Pallas kernels for 0%

profile of v1, /device:TPU:0, one launch (start us, length us, event | category | flops | bytes accessed | tf_op | source)
XLA Modules:
  0.0 901.9 jit_solution(3877934317788511689)
XLA Ops:
  7.2 0.7 reduce-scatter.2.cloned.1.call-update
  7.9 0.0 all-reduce.5.cloned.1.call-start
  8.0 285.6 %reduce-scatter.2.cloned.1.call-done = bf16[1024,2048]{1,0:T(8,128)(2,1)} async-done(((bf16[4096,2048]{1,0:T(8,128)(2,1)}), bf16[1024,2048]{1,0:T(8,128)(2,1)}) %reduce-scatter.2.cloned.1.call-update) | async-done | bytes 4194320 | tf_op jit(solution)/shard_map/reduce_scatter | solution.py:16
  293.5 17.7 %fusion.2 = f32[1024,384]{1,0:T(8,128)} fusion(f32[2048,384]{1,0:T(8,128)S(1)} %copy-done, f32[1024,2048]{1,0:T(8,128)} %param.4, bf16[1024,2048]{1,0:T(8,128)(2,1)} %reduce-scatter.2.cloned.1.call-done), kind=kOutput, calls=%fused_computation.8 | convolution fusion | flops 9669967872 | bytes 17301504 | tf_op jit(solution)/shard_map/dot_general | solution.py:20
  311.3 0.0 all-reduce.7.cloned.1.call-start
  311.3 43.6 %all-reduce.5.cloned.1.call-done = f32[1024,384]{1,0:T(8,128)} async-done(((f32[1024,384]{1,0:T(8,128)}), f32[1024,384]{1,0:T(8,128)}) %all-reduce.5.cloned.1.call-update) | async-done | bytes 1572880 | tf_op jit(solution)/shard_map/psum | solution.py:21
  354.9 1.6 multiply_reduce_fusion.1
  356.5 21.4 %psum.36 = f32[384]{0:T(512)S(1)} all-reduce(f32[384]{0:T(512)S(1)} %multiply_reduce_fusion.1), channel_id=1, replica_groups=mesh['rep'=4,'row'=2,'col'=4] {'rep','row'}, use_global_device_ids=true, to_apply=%region_3.0 | all-reduce | flops 384 | bytes 3072 | tf_op jit(solution)/shard_map/psum | solution.py:22
  377.9 0.6 multiply_sqrt_fusion
  378.5 5.6 fusion.8
  384.1 0.2 all-reduce.9.cloned.1.call-start
  384.3 0.1 fusion.7
  384.5 69.4 %all-reduce.7.cloned.1.call-done = f32[384,384]{0,1:T(8,128)} async-done(((f32[384,384]{0,1:T(8,128)}), f32[384,384]{0,1:T(8,128)}) %all-reduce.7.cloned.1.call-update) | async-done | bytes 589840 | tf_op jit(solution)/shard_map/psum | solution.py:25
  453.9 1.3 copy.8
  455.2 1.1 fusion.9
  456.3 11.7 %cholesky.77 = f32[128,128]{1,0:T(8,128)S(1)} custom-call(f32[128,128]{1,0:T(8,128)S(1)} %cholesky.192), custom_call_target="Cholesky" | custom-call | tf_op jit(solution)/shard_map/jit(cholesky)/cholesky | solution.py:26
  468.1 9.8 %custom-call.23 = f32[1,128,128]{1,2,0:T(8,128)S(1)} custom-call(f32[1,128,128]{2,1,0:T(8,128)S(1)} %get-tuple-element.28), custom_call_target="InvertDiagBlocksLowerTriangular" | custom-call | tf_op jit(solution)/shard_map/jit(cholesky)/cholesky | solution.py:26
  477.9 0.3 constant_dynamic-update-slice_fusion.10
  478.2 0.3 convolution_subtract_fusion.2
  478.5 11.7 %cholesky.162 = f32[128,128]{1,0:T(8,128)S(1)} custom-call(f32[128,128]{1,0:T(8,128)S(1)} %cholesky.196), custom_call_target="Cholesky" | custom-call | tf_op jit(solution)/shard_map/jit(cholesky)/cholesky | solution.py:26
  490.3 10.2 %custom-call.24 = f32[1,128,128]{1,2,0:T(8,128)S(1)} custom-call(f32[1,128,128]{2,1,0:T(8,128)S(1)} %get-tuple-element.25), custom_call_target="InvertDiagBlocksLowerTriangular" | custom-call | tf_op jit(solution)/shard_map/jit(cholesky)/cholesky | solution.py:26
  500.5 0.2 convolution_dynamic-update-slice_fusion
  500.7 0.3 convolution_subtract_fusion.3
  500.9 11.7 %cholesky.181 = f32[128,128]{1,0:T(8,128)S(1)} custom-call(f32[128,128]{1,0:T(8,128)S(1)} %convolution_subtract_fusion.3), custom_call_target="Cholesky" | custom-call | tf_op jit(solution)/shard_map/jit(cholesky)/cholesky | solution.py:26
  512.7 0.6 compare_reduce_fusion
  513.3 0.6 compare_reduce_fusion.1
  516.0 6.0 while.1
  516.0 0.1 constant_dynamic-slice_fusion.2
  516.1 0.5 fusion.41
  516.6 1.4 bitcast_dynamic-update-slice_fusion.2
  518.0 0.1 constant_dynamic-slice_fusion.2
  518.1 0.5 fusion.41
  518.6 1.4 bitcast_dynamic-update-slice_fusion.2
  520.0 0.1 constant_dynamic-slice_fusion.2
  520.0 0.5 fusion.41
  520.6 1.4 bitcast_dynamic-update-slice_fusion.2
  522.0 29.5 %custom-call.25 = f32[3,128,128]{1,2,0:T(8,128)S(1)} custom-call(f32[3,128,128]{2,1,0:T(8,128)S(1)} %get-tuple-element.11), custom_call_target="InvertDiagBlocksLowerTriangular" | custom-call | tf_op jit(solution)/shard_map/jit(_solve_triangular)/triangular_solve | solution.py:27
  551.5 0.6 fusion.10
  552.2 1.0 convolution_subtract_fusion.1
  553.2 0.6 fusion.18
  553.8 2.7 convolution_subtract_fusion
  556.5 0.6 fusion.16
  557.2 30.4 %fusion.1 = f32[2048,384]{1,0:T(8,128)} fusion(f32[1024,2048]{1,0:T(8,128)} %param.4, bf16[1024,2048]{1,0:T(8,128)(2,1)S(1)} %copy-done.2, f32[128,1024]{1,0:T(8,128)S(1)} %fusion.16, f32[128,1024]{1,0:T(8,128)S(1)} %fusion.18, f32[128,1024]{1,0:T(8,128)S(1)} %fusion.10), kind=kOutput, calls=%fused_computation.7 | convolution fusion | flops 9670754304 | bytes 17301504 | tf_op jit(solution)/shard_map/dot_general | solution.py:34
  587.6 0.1 fusion.6
  587.7 0.6 collective-permute-start
  588.3 66.8 %collective-permute-done = f32[1024,384]{0,1:T(8,128)S(1)} collective-permute-done((f32[1024,384]{0,1:T(8,128)S(1)}, f32[1024,384]{0,1:T(8,128)S(1)}, u32[]{:S(2)}, u32[]{:S(2)}) %collective-permute-start) | collective-permute-done | bytes 1572896 | tf_op jit(solution)/shard_map/ppermute | solution.py:30
  655.1 0.2 collective-permute-start.1
  655.3 108.5 %all-reduce.9.cloned.1.call-done = f32[2048,384]{1,0:T(8,128)} async-done(((f32[2048,384]{1,0:T(8,128)}), f32[2048,384]{1,0:T(8,128)}) %all-reduce.9.cloned.1.call-update) | async-done | bytes 3145744 | tf_op jit(solution)/shard_map/psum | solution.py:35
  763.8 2.2 multiply_reduce_fusion
  766.0 6.2 psum.39
  772.2 0.3 collective-permute-start.2
  772.5 2.3 broadcast_divide_fusion
  774.7 0.9 copy-done.3
  775.6 25.1 %multiply_subtract_fusion = f32[1024,2048]{1,0:T(8,128)} fusion(f32[2048,384]{1,0:T(8,128)} %all-reduce.9.cloned.1.call-done, f32[1024,2048]{1,0:T(8,128)} %param.4, bf16[1024,2048]{1,0:T(8,128)(2,1)S(1)} %copy-done.3, f32[128,1024]{1,0:T(8,128)S(1)} %fusion.16, f32[128,1024]{1,0:T(8,128)S(1)} %fusion.18, f32[128,1024]{1,0:T(8,128)S(1)} %fusion.10), kind=kOutput, calls=%fused_computation.3 | convolution fusion | flops 9674948608 | bytes 25690112 | tf_op jit(solution)/shard_map/dot_general | solution.py:38
  800.8 9.1 %collective-permute-done.2 = f32[1024,384]{0,1:T(8,128)S(1)} collective-permute-done((f32[1024,384]{0,1:T(8,128)}, f32[1024,384]{0,1:T(8,128)S(1)}, u32[]{:S(2)}, u32[]{:S(2)}) %collective-permute-start.2) | collective-permute-done | bytes 1572896 | tf_op jit(solution)/shard_map/ppermute | solution.py:30
  809.8 0.2 constant_dynamic-update-slice_fusion.7
  810.0 1.5 constant_dynamic-update-slice_fusion.6
  811.5 0.1 constant_dynamic-update-slice_fusion.5
  811.6 0.1 constant_dynamic-update-slice_fusion.4
  811.8 0.2 constant_dynamic-update-slice_fusion.3
  811.9 1.5 constant_dynamic-update-slice_fusion.2
  813.5 0.1 constant_dynamic-update-slice_fusion.1
  813.6 0.1 constant_dynamic-update-slice_fusion
  813.7 81.5 %multiply_convert_fusion = bf16[4096,2048]{1,0:T(8,128)(2,1)} fusion(f32[2048,384]{1,0:T(8,128)S(1)} %broadcast_divide_fusion, f32[8192,384]{0,1:T(8,128)S(1)} %constant_dynamic-update-slice_fusion, s32[]{:T(128)S(6)} %select_n.19), kind=kOutput, calls=%fused_computation.2 | convolution fusion | flops 38671482880 | bytes 26214404 | tf_op jit(solution)/shard_map/dot_general | solution.py:40
  (29 shorter events, 0.4 us)
Async XLA Ops:
  7.2 286.4 %copy-start = (f32[2048,384]{1,0:T(8,128)S(1)}, f32[2048,384]{1,0:T(8,128)}, u32[]{:S(2)}) copy-start(f32[2048,384]{1,0:T(8,128)} %param.5) | copy-start | bytes 9437188
  7.2 286.4 %reduce-scatter.2.cloned.1.call-start = ((), (), s32[]{:S(2)}) async-start(), calls=%async_computation.1 | async-start | bytes 20971520 | tf_op jit(solution)/shard_map/reduce_scatter | solution.py:16
  7.9 347.0 %all-reduce.5.cloned.1.call-start = ((), (), s32[]{:S(2)}) async-start(), calls=%async_computation.2 | async-start | bytes 3145728 | tf_op jit(solution)/shard_map/psum | solution.py:21
  311.3 142.6 %all-reduce.7.cloned.1.call-start = ((), (), s32[]{:S(2)}) async-start(), calls=%async_computation.3 | async-start | bytes 1179648 | tf_op jit(solution)/shard_map/psum | solution.py:25
  378.5 5.9 copy-start.4
  384.1 379.7 %all-reduce.9.cloned.1.call-start = ((), (), s32[]{:S(2)}) async-start(), calls=%async_computation.4 | async-start | bytes 6291456 | tf_op jit(solution)/shard_map/psum | solution.py:35
  522.0 30.2 %copy-start.6 = (f32[384,384]{1,0:T(8,128)}, f32[384,384]{1,0:T(8,128)S(1)}, u32[]{:S(2)}) copy-start(f32[384,384]{1,0:T(8,128)S(1)} %get-tuple-element.96) | copy-start | bytes 1769476
  552.1 5.0 copy-start.2
  587.7 67.4 %collective-permute-start = (f32[1024,384]{0,1:T(8,128)S(1)}, f32[1024,384]{0,1:T(8,128)S(1)}, u32[]{:S(2)}, u32[]{:S(2)}) collective-permute-start(f32[1024,384]{0,1:T(8,128)S(1)} %fusion.6), channel_id=1, source_target_pairs={{0,8},{8,16},{16,24},{24,0},{1,9},{9,17},{17,25},{25,1},{2,10},{10... | collective-permute-start | bytes 4718600 | tf_op jit(solution)/shard_map/ppermute | solution.py:30
  655.1 117.0 %collective-permute-start.1 = (f32[1024,384]{0,1:T(8,128)S(1)}, f32[1024,384]{0,1:T(8,128)}, u32[]{:S(2)}, u32[]{:S(2)}) collective-permute-start(f32[1024,384]{0,1:T(8,128)S(1)} %collective-permute-done), channel_id=1, source_target_pairs={{0,8},{8,16},{16,24},{24,0},{1,9},{9,17},{17,25},{25,1},{2,10},{10... | collective-permute-start | bytes 4718600 | tf_op jit(solution)/shard_map/ppermute | solution.py:30
  772.2 37.6 %collective-permute-start.2 = (f32[1024,384]{0,1:T(8,128)}, f32[1024,384]{0,1:T(8,128)S(1)}, u32[]{:S(2)}, u32[]{:S(2)}) collective-permute-start(f32[1024,384]{0,1:T(8,128)} %collective-permute-done.1), channel_id=1, source_target_pairs={{0,8},{8,16},{16,24},{24,0},{1,9},{9,17},{17,25},{25,1},{2,10},{10... | collective-permute-start | bytes 4718600 | tf_op jit(solution)/shard_map/ppermute | solution.py:30
  772.5 3.1 copy-start.3
  775.6 38.1 %copy-start.5 = (f32[2048,384]{1,0:T(8,128)}, f32[2048,384]{1,0:T(8,128)S(1)}, u32[]{:S(2)}) copy-start(f32[2048,384]{1,0:T(8,128)S(1)} %broadcast_divide_fusion) | copy-start | bytes 9437188
  813.7 81.5 %copy-start.1 = (f32[2048,384]{1,0:T(8,128)S(1)}, f32[2048,384]{1,0:T(8,128)}, u32[]{:S(2)}) copy-start(f32[2048,384]{1,0:T(8,128)} %param.5) | copy-start | bytes 9437188
Sparse Core Ops, SparseCore 0:
  10.3 283.1 reduce-scatter.1
  311.4 43.4 all-reduce.4
  384.2 69.6 all-reduce.6
  587.7 176.0 all-reduce.8
